TPU v7x, 32 devices: a whole 2x2x4 slice. The times are simulated.
32 devices in a mesh: role: 2 (over x), ctx: 4 (over z), head: 4 (over y, core).
Axes of the slice: x: 2, y: 2, z: 4, core: 2. Of those that a mesh axis runs over, the one named last changes fastest.
Arguments:
- tokens: bfloat16 [2, 256, 7168], P('role', 'ctx', 'head'), may hold values from -6 to 6
- latent_cache: bfloat16 [192, 576], P('ctx'), may hold values from -400 to 400
- offset: int32 [1], replicated, may hold values from 49 to 192
- bounds: int32 [256], P('ctx'), may hold values from 1 to 448
- query_down: bfloat16 [7168, 1536], P('head'), may hold values from -0.0625 to 0.0625
- latent_down_weight: bfloat16 [7168, 576], P('head'), may hold values from -0.0625 to 0.0625
- query_gain: float32 [1536], replicated, may hold values from 0.25 to 1.75
- latent_norm_gain: float32 [512], replicated, may hold values from 0.25 to 1.75
- query_up: bfloat16 [1536, 24576], P(None, 'head'), may hold values from -0.15625 to 0.15625
- key_up_transposed: bfloat16 [128, 128, 512], P('head'), may hold values from -0.5 to 0.5
- value_up_weight: bfloat16 [128, 512, 128], P('head'), may hold values from -0.25 to 0.25
Outputs:
- attended: bfloat16 [2, 256, 16384], P('role', 'ctx', 'head')
Inputs may be any that keep to these rules, and one draw needn't show every extreme that they name: `bounds`: A continuation row at position p sees keys at positions below p and itself. Cache slots from offset on are unused; the block's tokens sit at positions offset to offset + 255.
All inputs are finite; a program needn't handle non-finite values.
Results may differ from a plain program's by a relative error of at most 0.02.
Values may be sent and summed in bfloat16 or wider, within the bound.
No kernel may reach another device: no remote copies, remote signals or barrier semaphores. Data moves between devices by JAX's collectives and lax.ppermute only.
A program may use at most 128 MiB of HBM per device.

v0:
```python
import jax
import jax.numpy as jnp
from jax import lax
from jax.sharding import PartitionSpec as P

LATENT_WIDTH = 512
ROTARY_DIM = 64
PLAIN_QUERY_DIM = 128
VALUE_HEAD_SIZE = 128
EPS = 1e-06


def passed_along(value, axis, steps):
    count = lax.axis_size(axis)
    leading, last = (max(0, -steps), min(count, count - steps))
    return lax.ppermute(value, axis, [(source, source + steps) for source in range(leading, last)])


def root_mean_norm(value_rows, gain):
    return (
        value_rows
        * lax.rsqrt(jnp.mean(value_rows * value_rows, axis=-1, keepdims=True) + EPS)
        * gain
    )


def apply_rotary(value_rows, token_positions):
    half = value_rows.shape[-1] // 2
    freqs = 10000.0 ** (-jnp.arange(half, dtype=jnp.float32) / half)
    angles = token_positions.astype(jnp.float32)[:, None] * freqs[None, :]
    if value_rows.ndim == 3:
        angles = angles[:, None, :]
    first = value_rows[..., :half]
    second_half = value_rows[..., half:]
    cosine = jnp.cos(angles)
    sine = jnp.sin(angles)
    return jnp.concatenate(
        [first * cosine - second_half * sine, first * sine + second_half * cosine], axis=-1
    )


def finish_latents(query_lat, key_value_latent, token_positions, query_gain, latent_norm_gain):
    query_norm = root_mean_norm(query_lat, query_gain).astype(jnp.bfloat16)
    latent_vector = root_mean_norm(key_value_latent[:, :LATENT_WIDTH], latent_norm_gain)
    rotary_key_part = apply_rotary(key_value_latent[:, LATENT_WIDTH:], token_positions)
    return (
        query_norm,
        jnp.concatenate([latent_vector, rotary_key_part], axis=-1).astype(jnp.bfloat16),
    )


def local(
    tokens,
    latent_cache,
    offset,
    bounds,
    query_down,
    latent_down_weight,
    query_gain,
    latent_norm_gain,
    query_up,
    key_up_transposed,
    value_up_weight,
):
    count_of_rows = tokens.shape[1]
    cache_rows = latent_cache.shape[0]
    local_head_count = key_up_transposed.shape[0]
    role_index = lax.axis_index("role")
    block_start = offset[0]
    local_rows = lax.axis_index("ctx") * count_of_rows + jnp.arange(count_of_rows, dtype=jnp.int32)
    token_positions = jnp.where(role_index == 0, block_start + local_rows, bounds)
    inputs = tokens[0]
    query_part = jnp.dot(inputs, query_down, preferred_element_type=jnp.float32)
    kv_part = jnp.dot(inputs, latent_down_weight, preferred_element_type=jnp.float32)
    query_lat, key_value_latent = (
        lax.psum_scatter(query_part, "head", scatter_dimension=0, tiled=True),
        lax.psum_scatter(kv_part, "head", scatter_dimension=0, tiled=True),
    )
    share_rows = query_lat.shape[0]
    share_pos = lax.dynamic_slice_in_dim(
        token_positions, lax.axis_index("head") * share_rows, share_rows
    )
    query_share, key_share = finish_latents(
        query_lat, key_value_latent, share_pos, query_gain, latent_norm_gain
    )
    query_norm, self_key_row = (
        lax.all_gather(query_share, "head", axis=0, tiled=True),
        lax.all_gather(key_share, "head", axis=0, tiled=True),
    )
    queries = jnp.dot(query_norm, query_up, preferred_element_type=jnp.float32)
    queries = queries.reshape(count_of_rows, local_head_count, PLAIN_QUERY_DIM + ROTARY_DIM)
    query_nope = queries[..., :PLAIN_QUERY_DIM].astype(jnp.bfloat16)
    query_rot = apply_rotary(queries[..., PLAIN_QUERY_DIM:], token_positions).astype(jnp.bfloat16)
    absorbed = jnp.einsum(
        "rhn,hnc->rhc", query_nope, key_up_transposed, preferred_element_type=jnp.float32
    ).astype(jnp.bfloat16)
    complete_query = jnp.concatenate([absorbed, query_rot], axis=-1)
    softmax_scale = (PLAIN_QUERY_DIM + ROTARY_DIM) ** (-0.5)
    self_score = jnp.sum(
        complete_query.astype(jnp.float32) * self_key_row.astype(jnp.float32)[:, None, :], axis=-1
    )
    self_score = self_score.reshape(count_of_rows * local_head_count) * softmax_scale
    flattened_query = complete_query.reshape(
        count_of_rows * local_head_count, LATENT_WIDTH + ROTARY_DIM
    )
    row_limits = jnp.repeat(token_positions, local_head_count)
    relayed = passed_along(self_key_row, "role", 1)
    block_key = jnp.where(role_index == 0, self_key_row, relayed)
    per_shard = cache_rows + count_of_rows
    local_keys = jnp.concatenate([latent_cache, block_key], axis=0)
    slice_portion = lax.all_gather(local_keys, "ctx", axis=0, tiled=True)
    global_index = jnp.arange(slice_portion.shape[0], dtype=jnp.int32)
    shard_index = global_index // per_shard
    within = global_index % per_shard
    is_cached = within < cache_rows
    key_pos = jnp.where(
        is_cached,
        shard_index * cache_rows + within,
        block_start + shard_index * count_of_rows + within - cache_rows,
    )
    key_valid = jnp.where(is_cached, key_pos < block_start, True)
    running_max = self_score
    running_sum = jnp.ones_like(self_score)
    output_accumulate = jnp.repeat(
        self_key_row[:, :LATENT_WIDTH].astype(jnp.float32), local_head_count, axis=0
    )
    scores = (
        jnp.dot(flattened_query, slice_portion.T, preferred_element_type=jnp.float32)
        * softmax_scale
    )
    key_mask = key_valid[None, :] & (key_pos[None, :] < row_limits[:, None])
    new_max = jnp.maximum(running_max, jnp.max(jnp.where(key_mask, scores, -jnp.inf), axis=-1))
    attention_weights = jnp.where(key_mask, jnp.exp(scores - new_max[:, None]), 0.0)
    fading = jnp.exp(running_max - new_max)
    running_sum = running_sum * fading + jnp.sum(attention_weights, axis=-1)
    output_accumulate = output_accumulate * fading[:, None] + jnp.dot(
        attention_weights.astype(jnp.bfloat16),
        slice_portion[:, :LATENT_WIDTH],
        preferred_element_type=jnp.float32,
    )
    final_state = (new_max, running_sum, output_accumulate)
    running_max, running_sum, output_accumulate = final_state
    out_latent = (
        (output_accumulate / running_sum[:, None])
        .astype(jnp.bfloat16)
        .reshape(count_of_rows, local_head_count, LATENT_WIDTH)
    )
    result = jnp.einsum(
        "rhc,hcv->rhv", out_latent, value_up_weight, preferred_element_type=jnp.float32
    ).astype(jnp.bfloat16)
    return result.reshape(1, count_of_rows, local_head_count * VALUE_HEAD_SIZE)


def solution(mesh):
    return jax.shard_map(
        local,
        mesh=mesh,
        in_specs=(
            P("role", "ctx", "head"),
            P("ctx", None),
            P(),
            P("ctx"),
            P("head", None),
            P("head", None),
            P(),
            P(),
            P(None, "head"),
            P("head", None, None),
            P("head", None, None),
        ),
        out_specs=P("role", "ctx", "head"),
        check_vma=False,
    )
```

profile of v0, /device:TPU:11, one launch (start us, length us, event | category | flops | bytes accessed | tf_op | source)
XLA Modules:
  0.0 112.0 jit_solution(4370328223607558288)
XLA Ops:
  6.5 1.6 %copy-done = bf16[1792,576]{0,1:T(8,128)(2,1)S(1)} copy-done((bf16[1792,576]{0,1:T(8,128)(2,1)S(1)}, bf16[1792,576]{0,1:T(8,128)(2,1)}, u32[]{:S(2)}) %copy-start) | copy-done | bytes 2064408
  8.1 2.3 %fusion.23 = f32[64,576]{1,0:T(8,128)} fusion(bf16[1792,576]{0,1:T(8,128)(2,1)S(1)} %copy-done, bf16[1,64,1792]{2,1,0:T(8,128)(2,1)} %param.11), kind=kOutput, calls=%fused_computation.28 | convolution fusion | flops 132120576 | bytes 2441216 | tf_op jit(solution)/shard_map/dot_general | solution.py:74
  10.5 4.5 %fusion.21 = f32[64,1536]{1,0:T(8,128)} fusion(bf16[1792,1536]{1,0:T(8,128)(2,1)} %param.15, bf16[1,64,1792]{2,1,0:T(8,128)(2,1)} %param.11), kind=kOutput, calls=%fused_computation.26 | convolution fusion | flops 352321536 | bytes 6127616 | tf_op jit(solution)/shard_map/dot_general | solution.py:73
  16.3 14.8 %reduce-scatter.3.cloned.1.call-done = f32[16,576]{1,0:T(8,128)} async-done(((f32[64,576]{1,0:T(8,128)}), f32[16,576]{1,0:T(8,128)}) %reduce-scatter.3.cloned.1.call-update) | async-done | bytes 36880 | tf_op jit(solution)/shard_map/reduce_scatter | solution.py:77
  31.9 0.9 fusion.30
  33.7 6.2 %all_gather.9 = bf16[64,576]{1,0:T(8,128)(2,1)S(1)} all-gather(bf16[16,576]{1,0:T(8,128)(2,1)S(1)} %pad_maximum_fusion.2), channel_id=1, replica_groups=mesh['role'=2,'ctx'=4,'head'=4] {'head'}, dimensions={0}, use_global_device_ids=true | all-gather | bytes 92160 | tf_op jit(solution)/shard_map/all_gather | solution.py:88
  39.9 1.3 %collective-permute-start = (bf16[64,576]{1,0:T(8,128)(2,1)S(1)}, bf16[64,576]{1,0:T(8,128)(2,1)S(1)}, u32[]{:S(2)}, u32[]{:S(2)}) collective-permute-start(bf16[64,576]{1,0:T(8,128)(2,1)S(1)} %all_gather.9), channel_id=1, source_target_pairs={{0,16},{1,17},{2,18},{3,19},{4,20},{5,21},{6,22},{7,23},{8,24},{9,... | collective-permute-start | bytes 221192 | tf_op jit(solution)/shard_map/ppermute | solution.py:16
  41.3 4.4 %collective-permute-done = bf16[64,576]{1,0:T(8,128)(2,1)S(1)} collective-permute-done((bf16[64,576]{1,0:T(8,128)(2,1)S(1)}, bf16[64,576]{1,0:T(8,128)(2,1)S(1)}, u32[]{:S(2)}, u32[]{:S(2)}) %collective-permute-start) | collective-permute-done | bytes 73760 | tf_op jit(solution)/shard_map/ppermute | solution.py:16
  45.7 12.4 %all_gather.11 = bf16[448,576]{1,0:T(8,128)(2,1)S(1)} all-gather(bf16[112,576]{1,0:T(8,128)(2,1)S(1)} %pad_maximum_fusion.1), channel_id=1, replica_groups=mesh['role'=2,'ctx'=4,'head'=4] {'ctx'}, dimensions={0}, use_global_device_ids=true | all-gather | bytes 645120 | tf_op jit(solution)/shard_map/all_gather | solution.py:111
  58.1 1.0 multiply_reduce_fusion.1
  59.2 1.0 multiply_convert_fusion
  60.1 10.5 %all_gather.10 = bf16[64,1536]{1,0:T(8,128)(2,1)S(1)} all-gather(bf16[16,1536]{1,0:T(8,128)(2,1)S(1)} %multiply_convert_fusion), channel_id=1, replica_groups=mesh['role'=2,'ctx'=4,'head'=4] {'head'}, dimensions={0}, use_global_device_ids=true | all-gather | bytes 245760 | tf_op jit(solution)/shard_map/all_gather | solution.py:87
  70.6 11.0 %fusion.44 = f32[64,6144]{1,0:T(8,128)} fusion(bf16[64,1536]{1,0:T(8,128)(2,1)S(1)} %all_gather.10, bf16[1536,6144]{1,0:T(8,128)(2,1)} %param.19), kind=kOutput, calls=%fused_computation.75 | convolution fusion | flops 1207959552 | bytes 20643840 | tf_op jit(solution)/shard_map/dot_general | solution.py:90
  81.7 3.1 %reshape.145 = f32[64,32,192]{2,1,0:T(8,128)} reshape(f32[64,6144]{1,0:T(8,128)} %fusion.44) | data formatting | bytes 3145728 | tf_op jit(solution)/shard_map/reshape | solution.py:91
  84.8 2.1 %fusion.43 = (f32[64,32,32]{2,1,0:T(8,128)S(1)}, f32[64,32,32]{2,1,0:T(8,128)S(1)}) fusion(f32[64,32,192]{2,1,0:T(8,128)} %reshape.145), kind=kLoop, calls=%fused_computation.74 | loop fusion | bytes 1048576 | tf_op jit(solution)/shard_map/slice | solution.py:33
  86.9 1.3 %slice.43 = bf16[64,32,128]{2,1,0:T(8,128)(2,1)S(1)} slice(f32[64,32,192]{2,1,0:T(8,128)} %reshape.145), slice={[0:64], [0:32], [0:128]} | slice | bytes 1048576 | tf_op jit(solution)/shard_map/slice | solution.py:92
  88.9 1.2 %subtract_convert_fusion = (bf16[64,32,32]{2,0,1:T(8,128)(2,1)S(1)}, bf16[64,32,32]{2,0,1:T(8,128)(2,1)S(1)}) fusion(f32[64,32,32]{2,1,0:T(8,128)S(1)} %get-tuple-element.14, f32[64,32,32]{2,1,0:T(8,128)S(1)} %get-tuple-element.13, f32[64,32]{1,0:T(8,128)S(1)} %get-tuple-element.20, f32[64,32]{1,0:T(8,128)S(1)} %get-tuple-element.19), kind=kLoop, calls=%fused_computation.24 | loop fusion | flops 524288 | bytes 802816 | tf_op jit(solution)/shard_map/convert
  90.2 0.9 multiply_reduce_fusion
  91.1 3.0 %copy.26 = bf16[64,32,576]{2,1,0:T(8,128)(2,1)} copy(bf16[64,32,576]{2,0,1:T(8,128)(2,1)S(1)} %get-tuple-element.8) | data formatting | bytes 4718592 | tf_op jit(solution)/shard_map/concatenate | solution.py:97
  94.3 3.6 %select_reduce_fusion = (f32[2048]{0:T(1024)S(1)}, f32[2048,448]{0,1:T(8,128)S(1)}) fusion(s32[2048]{0:T(1024)S(1)} %lt.55, s32[448]{0:T(512)S(1)} %add_select_fusion.2, pred[448]{0:T(512)(128)(4,1)S(1)} %compare_select_fusion, bf16[2048,576]{1,0:T(8,128)(2,1)} %bitcast.32, bf16[448,576]{1,0:T(8,128)(2,1)S(1)} %all_gather.11), kind=kOutput, calls=%fused_computation.6 | convolution fusion | flops 1061550080 | bytes 6564032 | tf_op jit(solution)/shard_map/dot_general | solution.py:128
  97.8 1.2 %fusion.3 = f32[2048]{0:T(1024)S(1)} fusion(f32[2048,448]{0,1:T(8,128)S(1)} %get-tuple-element.22, f32[2048]{0:T(1024)S(1)} %max.13, s32[2048]{0:T(1024)S(1)} %lt.55, s32[448]{0:T(512)S(1)} %add_select_fusion.2, pred[448]{0:T(512)(128)(4,1)S(1)} %compare_select_fusion), kind=kLoop, calls=%fused_computation.9 | loop fusion | flops 5502976 | bytes 3696832 | tf_op jit(solution)/shard_map/reduce_sum | solution.py:135
  99.1 2.0 %fusion.2 = bf16[2048,512]{1,0:T(8,128)(2,1)S(1)} fusion(f32[2048]{0:T(1024)S(1)} %get-tuple-element.5, f32[2048]{0:T(1024)S(1)} %get-tuple-element.6, f32[64,512]{1,0:T(8,128)S(1)} %slice_convert_fusion, f32[2048,448]{0,1:T(8,128)S(1)} %get-tuple-element.22, f32[2048]{0:T(1024)S(1)} %max.13, s32[2048]{0:T(1024)S(1)} %lt.55, s32[448]{0:T(512)S(1)} %add_select_fusion.2, ...), kind=kOutput, calls=%fused_computation.4 | convolution fusion | flops 949223424 | bytes 6392320 | tf_op jit(solution)/shard_map/dot_general | solution.py:136
  101.3 2.5 %fusion.17 = bf16[64,32,128]{2,0,1:T(8,128)(2,1)S(1)} fusion(bf16[32,512,128]{2,1,0:T(8,128)(2,1)S(1)} %copy-done.2, bf16[64,32,512]{2,1,0:T(8,128)(2,1)S(1)} %bitcast.31), kind=kOutput, calls=%fused_computation.21 | convolution fusion | flops 268697600 | bytes 6815744 | tf_op jit(solution)/shard_map/rhc,hcv->rhv/dot_general | solution.py:148
  104.2 1.0 reshape.148
  (41 shorter events, 3.9 us)
Async XLA Ops:
  6.5 1.6 %copy-start = (bf16[1792,576]{0,1:T(8,128)(2,1)S(1)}, bf16[1792,576]{0,1:T(8,128)(2,1)}, u32[]{:S(2)}) copy-start(bf16[1792,576]{0,1:T(8,128)(2,1)} %param.16) | copy-start | bytes 6193156
  6.5 24.5 %reduce-scatter.3.cloned.1.call-start = ((), (), s32[]{:S(2)}) async-start(), calls=%async_computation.2 | async-start | bytes 204800 | tf_op jit(solution)/shard_map/reduce_scatter | solution.py:77
  10.4 5.3 %copy-start.6 = (s32[64]{0:T(128)S(1)}, s32[64]{0:T(128)}, u32[]{:S(2)}) copy-start(s32[64]{0:T(128)} %param.14) | copy-start | bytes 772
  10.4 22.4 %copy-start.5 = (f32[512]{0:T(512)S(1)}, f32[512]{0:T(512)}, u32[]{:S(2)}) copy-start(f32[512]{0:T(512)} %param.18) | copy-start | bytes 6148
  10.5 35.2 %copy-start.3 = (bf16[48,576]{1,0:T(8,128)(2,1)S(1)}, bf16[48,576]{1,0:T(8,128)(2,1)}, u32[]{:S(2)}) copy-start(bf16[48,576]{1,0:T(8,128)(2,1)} %param.12) | copy-start | bytes 165892
  10.5 48.7 %copy-start.4 = (f32[1536]{0:T(1024)S(1)}, f32[1536]{0:T(1024)}, u32[]{:S(2)}) copy-start(f32[1536]{0:T(1024)} %param.17) | copy-start | bytes 18436
  10.5 47.6 %reduce-scatter.5.cloned.1.call-start = ((), (), s32[]{:S(2)}) async-start(), calls=%async_computation.3 | async-start | bytes 491520 | tf_op jit(solution)/shard_map/reduce_scatter | solution.py:76
  39.9 5.7 %collective-permute-start = (bf16[64,576]{1,0:T(8,128)(2,1)S(1)}, bf16[64,576]{1,0:T(8,128)(2,1)S(1)}, u32[]{:S(2)}, u32[]{:S(2)}) collective-permute-start(bf16[64,576]{1,0:T(8,128)(2,1)S(1)} %all_gather.9), channel_id=1, source_target_pairs={{0,16},{1,17},{2,18},{3,19},{4,20},{5,21},{6,22},{7,23},{8,24},{9,... | collective-permute-start | bytes 221192 | tf_op jit(solution)/shard_map/ppermute | solution.py:16
  84.8 3.4 %copy-start.1 = (bf16[32,128,512]{2,1,0:T(8,128)(2,1)S(1)}, bf16[32,128,512]{2,1,0:T(8,128)(2,1)}, u32[]{:S(2)}) copy-start(bf16[32,128,512]{2,1,0:T(8,128)(2,1)} %param.20) | copy-start | bytes 12582916
  99.1 2.2 %copy-start.2 = (bf16[32,512,128]{2,1,0:T(8,128)(2,1)S(1)}, bf16[32,512,128]{2,1,0:T(8,128)(2,1)}, u32[]{:S(2)}) copy-start(bf16[32,512,128]{2,1,0:T(8,128)(2,1)} %param.21) | copy-start | bytes 12582916
Sparse Core Ops, SparseCore 0:
  10.6 20.3 reduce-scatter.2
  33.5 21.1 reduce-scatter.4
where the time goes:
time: 113 us; the launch traced here: 112 us
  blocking collectives  29.1 us (26%)
  matrix products  26.7 us (24%)
  waiting for transfers between devices  19.2 us (17%)
  between operations  14.3 us (13%)
  local copies, waits for them, and re-layouts  13 us (12%)
  other arithmetic  8.49 us (8%)
  starting transfers between devices  1.32 us (1%)
    reduce_scatter x1, waiting for transfers between devices, local(): lax.psum_scatter(kv_part, 'head', scatter_dimension=0, tiled=True)  14.8 us
    all_gather x1, blocking collectives, local(): slice_portion = lax.all_gather(local_keys, 'ctx', axis=0, tiled=True)  12.4 us
    dot_general x1, matrix products, local(): queries = jnp.dot(query_norm, query_up, preferred_element_type=jnp.float32)  11 us
    all_gather x1, blocking collectives, local(): lax.all_gather(query_share, 'head', axis=0, tiled=True)  10.5 us
    all_gather x1, blocking collectives, local(): lax.all_gather(key_share, 'head', axis=0, tiled=True)  6.22 us
    dot_general x1, matrix products, local(): query_part = jnp.dot(inputs, query_down, preferred_element_type=jnp.float32)  4.52 us
    ppermute x1, waiting for transfers between devices, passed_along(): lax.ppermute(value, axis, [(source, source + steps) for source in range(l...  4.41 us
    dot_general x1, matrix products, local(): jnp.dot(flattened_query, slice_portion.T, preferred_element_type=jnp.floa...  3.55 us
  transfers between devices with their start and end apart: 3, of which 2 were waited for; matrix products, arithmetic and copies ran while one was open for 7% of the time, Pallas kernels for 0%

commit v1 on v0

--- a/solution.py
+++ b/solution.py
@@ -8,6 +8,19 @@
 PLAIN_QUERY_DIM = 128
 VALUE_HEAD_SIZE = 128
 EPS = 1e-06
+
+
+def ring_gather(x, axis, dim):
+    ways = lax.axis_size(axis)
+    up = [(d, (d + 1) % ways) for d in range(ways)]
+    down = [(d, (d - 1) % ways) for d in range(ways)]
+    earlier, later = ([x], [x])
+    for _ in range(ways // 2):
+        earlier.append(lax.ppermute(earlier[-1], axis, up))
+    for _ in range((ways - 1) // 2):
+        later.append(lax.ppermute(later[-1], axis, down))
+    line = jnp.concatenate([*earlier[::-1], *later[1:]], axis=dim)
+    return jnp.roll(line, (lax.axis_index(axis) - ways // 2) * x.shape[dim], axis=dim)
 
 
 def passed_along(value, axis, steps):
@@ -85,7 +98,7 @@
     )
     query_norm, self_key_row = (
         lax.all_gather(query_share, "head", axis=0, tiled=True),
-        lax.all_gather(key_share, "head", axis=0, tiled=True),
+        ring_gather(key_share, "head", 0),
     )
     queries = jnp.dot(query_norm, query_up, preferred_element_type=jnp.float32)
     queries = queries.reshape(count_of_rows, local_head_count, PLAIN_QUERY_DIM + ROTARY_DIM)

time: 113 us -> 115 us (1.018)
  blocking collectives: 29.1 us -> 22.6 us
  waiting for transfers between devices: 19.2 us -> 23.7 us
  starting transfers between devices: 1.32 us -> 4.94 us
  matrix products: 26.7 us -> 24.9 us
  other arithmetic: 8.49 us -> 10.1 us
    all_gather x1 -> x0, blocking collectives: 6.22 us -> none  [local(): lax.all_gather(key_share, 'head', axis=0, tiled=True)]
    ppermute x0 -> x3, waiting for transfers between devices: none -> 3.99 us  [the longest x1 2.39 us: ring_gather(): later.append(lax.ppermute(later[-1], axis, down))]
    ppermute x0 -> x3, starting transfers between devices: none -> 3.6 us  [the longest x2 3.6 us: ring_gather(): earlier.append(lax.ppermute(earlier[-1], axis, up))]
    dot_general x1, matrix products: 3.55 us -> 1.81 us  [local(): jnp.dot(flattened_query, slice_portion.T, preferred_element_type=jnp.floa...]
    reduce_sum x1, other arithmetic: 0.92 us -> 2.35 us  [local(): jnp.sum(complete_query.astype(jnp.float32) * self_key_row.astype(jnp.floa...]
  transfers between devices with their start and end apart: 3 -> 6, of which waited for: 2 -> 5; matrix products, arithmetic and copies ran while one was open for 7% -> 7% of each run, Pallas kernels for 0% -> 0%
where the time goes in v1:
time: 115 us; the launch traced here: 114 us
  matrix products  24.9 us (22%)
  waiting for transfers between devices  23.7 us (21%)
  blocking collectives  22.6 us (20%)
  between operations  14.3 us (12%)
  local copies, waits for them, and re-layouts  13.4 us (12%)
  other arithmetic  10.1 us (9%)
  starting transfers between devices  4.94 us (4%)
    reduce_scatter x1, waiting for transfers between devices, local(): lax.psum_scatter(kv_part, 'head', scatter_dimension=0, tiled=True)  14.9 us
    all_gather x1, blocking collectives, local(): slice_portion = lax.all_gather(local_keys, 'ctx', axis=0, tiled=True)  12.8 us
    dot_general x1, matrix products, local(): queries = jnp.dot(query_norm, query_up, preferred_element_type=jnp.float32)  11 us
    all_gather x1, blocking collectives, local(): lax.all_gather(query_share, 'head', axis=0, tiled=True)  9.84 us
    ppermute x1, waiting for transfers between devices, passed_along(): lax.ppermute(value, axis, [(source, source + steps) for source in range(l...  4.72 us
    dot_general x1, matrix products, local(): query_part = jnp.dot(inputs, query_down, preferred_element_type=jnp.float32)  4.52 us
    ppermute x2, starting transfers between devices, ring_gather(): earlier.append(lax.ppermute(earlier[-1], axis, up))  3.6 us
    concatenate x1, local copies, waits for them, and re-layouts, local(): complete_query = jnp.concatenate([absorbed, query_rot], axis=-1)  3.24 us
  transfers between devices with their start and end apart: 6, of which 5 were waited for; matrix products, arithmetic and copies ran while one was open for 7% of the time, Pallas kernels for 0%

profile of v1, /device:TPU:11, one launch (start us, length us, event | category | flops | bytes accessed | tf_op | source)
XLA Modules:
  0.0 113.9 jit_solution(10646808280714123797)
XLA Ops:
  6.5 1.6 %copy-done = bf16[1792,576]{0,1:T(8,128)(2,1)S(1)} copy-done((bf16[1792,576]{0,1:T(8,128)(2,1)S(1)}, bf16[1792,576]{0,1:T(8,128)(2,1)}, u32[]{:S(2)}) %copy-start) | copy-done | bytes 2064408
  8.1 2.3 %fusion.24 = f32[64,576]{1,0:T(8,128)} fusion(bf16[1792,576]{0,1:T(8,128)(2,1)S(1)} %copy-done, bf16[1,64,1792]{2,1,0:T(8,128)(2,1)} %param.11), kind=kOutput, calls=%fused_computation.29 | convolution fusion | flops 132120576 | bytes 2441216 | tf_op jit(solution)/shard_map/dot_general | solution.py:87
  10.6 4.5 %fusion.22 = f32[64,1536]{1,0:T(8,128)} fusion(bf16[1792,1536]{1,0:T(8,128)(2,1)} %param.15, bf16[1,64,1792]{2,1,0:T(8,128)(2,1)} %param.11), kind=kOutput, calls=%fused_computation.27 | convolution fusion | flops 352321536 | bytes 6127616 | tf_op jit(solution)/shard_map/dot_general | solution.py:86
  16.1 14.9 %reduce-scatter.3.cloned.1.call-done = f32[16,576]{1,0:T(8,128)} async-done(((f32[64,576]{1,0:T(8,128)}), f32[16,576]{1,0:T(8,128)}) %reduce-scatter.3.cloned.1.call-update) | async-done | bytes 36880 | tf_op jit(solution)/shard_map/reduce_scatter | solution.py:90
  33.7 1.3 %collective-permute-start = (bf16[16,576]{1,0:T(8,128)(2,1)S(1)}, bf16[16,576]{1,0:T(8,128)(2,1)S(1)}, u32[]{:S(2)}, u32[]{:S(2)}) collective-permute-start(bf16[16,576]{1,0:T(8,128)(2,1)S(1)} %pad_maximum_fusion.2), channel_id=1, source_target_pairs={{0,1},{1,2},{2,3},{3,0},{4,5},{5,6},{6,7},{7,4},{8,9},{9,10},{10,1... | collective-permute-start | bytes 55304 | tf_op jit(solution)/shard_map/ppermute | solution.py:19
  35.9 2.3 %collective-permute-start.1 = (bf16[16,576]{1,0:T(8,128)(2,1)S(1)}, bf16[16,576]{1,0:T(8,128)(2,1)S(1)}, u32[]{:S(2)}, u32[]{:S(2)}) collective-permute-start(bf16[16,576]{1,0:T(8,128)(2,1)S(1)} %collective-permute-done), channel_id=1, source_target_pairs={{0,1},{1,2},{2,3},{3,0},{4,5},{5,6},{6,7},{7,4},{8,9},{9,10},{10,1... | collective-permute-start | bytes 55304 | tf_op jit(solution)/shard_map/ppermute | solution.py:19
  39.2 2.4 %collective-permute-done.2 = bf16[16,576]{1,0:T(8,128)(2,1)S(1)} collective-permute-done((bf16[16,576]{1,0:T(8,128)(2,1)S(1)}, bf16[16,576]{1,0:T(8,128)(2,1)S(1)}, u32[]{:S(2)}, u32[]{:S(2)}) %collective-permute-start.2) | collective-permute-done | bytes 18464 | tf_op jit(solution)/shard_map/ppermute | solution.py:21
  41.8 1.3 %collective-permute-start.3 = (bf16[64,576]{1,0:T(8,128)(2,1)S(1)}, bf16[64,576]{1,0:T(8,128)(2,1)S(1)}, u32[]{:S(2)}, u32[]{:S(2)}) collective-permute-start(bf16[64,576]{1,0:T(8,128)(2,1)S(1)} %get-tuple-element.10), channel_id=1, source_target_pairs={{0,16},{1,17},{2,18},{3,19},{4,20},{5,21},{6,22},{7,23},{8,24},{9,... | collective-permute-start | bytes 221192 | tf_op jit(solution)/shard_map/ppermute | solution.py:29
  43.1 4.7 %collective-permute-done.3 = bf16[64,576]{1,0:T(8,128)(2,1)S(1)} collective-permute-done((bf16[64,576]{1,0:T(8,128)(2,1)S(1)}, bf16[64,576]{1,0:T(8,128)(2,1)S(1)}, u32[]{:S(2)}, u32[]{:S(2)}) %collective-permute-start.3) | collective-permute-done | bytes 73760 | tf_op jit(solution)/shard_map/ppermute | solution.py:29
  47.9 12.8 %all_gather.7 = bf16[448,576]{1,0:T(8,128)(2,1)S(1)} all-gather(bf16[112,576]{1,0:T(8,128)(2,1)S(1)} %pad_maximum_fusion.1), channel_id=1, replica_groups=mesh['role'=2,'ctx'=4,'head'=4] {'ctx'}, dimensions={0}, use_global_device_ids=true | all-gather | bytes 645120 | tf_op jit(solution)/shard_map/all_gather | solution.py:124
  60.6 1.0 multiply_reduce_fusion.1
  62.7 9.8 %all_gather.6 = bf16[64,1536]{1,0:T(8,128)(2,1)S(1)} all-gather(bf16[16,1536]{1,0:T(8,128)(2,1)S(1)} %multiply_convert_fusion), channel_id=1, replica_groups=mesh['role'=2,'ctx'=4,'head'=4] {'head'}, dimensions={0}, use_global_device_ids=true | all-gather | bytes 245760 | tf_op jit(solution)/shard_map/all_gather | solution.py:100
  72.5 11.0 %fusion.46 = f32[64,6144]{1,0:T(8,128)} fusion(bf16[64,1536]{1,0:T(8,128)(2,1)S(1)} %all_gather.6, bf16[1536,6144]{1,0:T(8,128)(2,1)} %param.19), kind=kOutput, calls=%fused_computation.86 | convolution fusion | flops 1207959552 | bytes 20643840 | tf_op jit(solution)/shard_map/dot_general | solution.py:103
  83.5 3.1 %reshape.145 = f32[64,32,192]{2,1,0:T(8,128)} reshape(f32[64,6144]{1,0:T(8,128)} %fusion.46) | data formatting | bytes 3145728 | tf_op jit(solution)/shard_map/reshape | solution.py:104
  86.7 1.5 %slice.42 = bf16[64,32,128]{2,1,0:T(8,128)(2,1)S(1)} slice(f32[64,32,192]{2,1,0:T(8,128)} %reshape.145), slice={[0:64], [0:32], [0:128]} | slice | bytes 1048576 | tf_op jit(solution)/shard_map/slice | solution.py:105
  88.2 2.0 %fusion.45 = (f32[64,32,32]{2,1,0:T(8,128)S(1)}, f32[64,32,32]{2,1,0:T(8,128)S(1)}) fusion(f32[64,32,192]{2,1,0:T(8,128)} %reshape.145), kind=kLoop, calls=%fused_computation.85 | loop fusion | bytes 1048576 | tf_op jit(solution)/shard_map/slice | solution.py:46
  90.9 1.2 %subtract_convert_fusion = (bf16[64,32,32]{2,0,1:T(8,128)(2,1)S(1)}, bf16[64,32,32]{2,0,1:T(8,128)(2,1)S(1)}) fusion(f32[64,32,32]{2,1,0:T(8,128)S(1)} %get-tuple-element.16, f32[64,32,32]{2,1,0:T(8,128)S(1)} %get-tuple-element.15, f32[64,32]{1,0:T(8,128)S(1)} %get-tuple-element.20, f32[64,32]{1,0:T(8,128)S(1)} %get-tuple-element.19), kind=kLoop, calls=%fused_computation.25 | loop fusion | flops 524288 | bytes 802816 | tf_op jit(solution)/shard_map/convert
  92.2 2.4 %multiply_reduce_fusion = (f32[64,32]{0,1:T(8,128)S(1)}, bf16[64,32,576]{2,0,1:T(8,128)(2,1)}) fusion(f32[64,576]{1,0:T(8,128)S(1)} %get-tuple-element.9, bf16[64,32,32]{2,0,1:T(8,128)(2,1)S(1)} %get-tuple-element.14, bf16[64,32,32]{2,0,1:T(8,128)(2,1)S(1)} %get-tuple-element.13, bf16[64,32,512]{2,0,1:T(8,128)(2,1)S(1)} %convert_bitcast_fusion), kind=kLoop, calls=%fused_computation | loop fusion | flops 10614784 | bytes 4874240 | tf_op jit(solution)/shard_map/reduce_sum | solution.py:112
  94.7 3.2 %copy.26 = bf16[64,32,576]{2,1,0:T(8,128)(2,1)S(1)} copy(bf16[64,32,576]{2,0,1:T(8,128)(2,1)} %get-tuple-element.8) | data formatting | bytes 4718592 | tf_op jit(solution)/shard_map/concatenate | solution.py:110
  97.9 1.8 %select_reduce_fusion = (f32[2048]{0:T(1024)S(1)}, f32[2048,448]{0,1:T(8,128)S(1)}) fusion(s32[2048]{0:T(1024)S(1)} %lt.69, s32[448]{0:T(512)S(1)} %add_select_fusion.2, pred[448]{0:T(512)(128)(4,1)S(1)} %compare_select_fusion, bf16[2048,576]{1,0:T(8,128)(2,1)S(1)} %bitcast.32, bf16[448,576]{1,0:T(8,128)(2,1)S(1)} %all_gather.7), kind=kOutput, calls=%fused_computation.6 | convolution fusion | flops 1061550080 | bytes 6564032 | tf_op jit(solution)/shard_map/dot_general | solution.py:141
  99.8 1.2 %fusion.3 = f32[2048]{0:T(1024)S(1)} fusion(f32[2048,448]{0,1:T(8,128)S(1)} %get-tuple-element.22, f32[2048]{0:T(1024)S(1)} %max.13, s32[2048]{0:T(1024)S(1)} %lt.69, s32[448]{0:T(512)S(1)} %add_select_fusion.2, pred[448]{0:T(512)(128)(4,1)S(1)} %compare_select_fusion), kind=kLoop, calls=%fused_computation.9 | loop fusion | flops 5502976 | bytes 3696832 | tf_op jit(solution)/shard_map/reduce_sum | solution.py:148
  101.0 2.0 %fusion.2 = bf16[2048,512]{1,0:T(8,128)(2,1)S(1)} fusion(f32[2048]{0:T(1024)S(1)} %get-tuple-element.5, f32[2048]{0:T(1024)S(1)} %get-tuple-element.6, f32[64,512]{1,0:T(8,128)S(1)} %dynamic-slice_convert_fusion, bf16[448,576]{1,0:T(8,128)(2,1)S(1)} %all_gather.7, f32[2048,448]{0,1:T(8,128)S(1)} %get-tuple-element.22, f32[2048]{0:T(1024)S(1)} %max.13, ...), kind=kOutput, calls=%fused_computation.4 | convolution fusion | flops 949223424 | bytes 6392320 | tf_op jit(solution)/shard_map/dot_general | solution.py:149
  103.2 2.5 %fusion.18 = bf16[64,32,128]{2,0,1:T(8,128)(2,1)S(1)} fusion(bf16[32,512,128]{2,1,0:T(8,128)(2,1)S(1)} %copy-done.2, bf16[64,32,512]{2,1,0:T(8,128)(2,1)S(1)} %bitcast.31), kind=kOutput, calls=%fused_computation.22 | convolution fusion | flops 268697600 | bytes 6815744 | tf_op jit(solution)/shard_map/rhc,hcv->rhv/dot_general | solution.py:161
  106.1 1.0 reshape.148
  (55 shorter events, 7.6 us)
Async XLA Ops:
  6.5 1.6 %copy-start = (bf16[1792,576]{0,1:T(8,128)(2,1)S(1)}, bf16[1792,576]{0,1:T(8,128)(2,1)}, u32[]{:S(2)}) copy-start(bf16[1792,576]{0,1:T(8,128)(2,1)} %param.16) | copy-start | bytes 6193156
  6.5 24.5 %reduce-scatter.3.cloned.1.call-start = ((), (), s32[]{:S(2)}) async-start(), calls=%async_computation.2 | async-start | bytes 204800 | tf_op jit(solution)/shard_map/reduce_scatter | solution.py:90
  10.4 5.3 %copy-start.6 = (s32[64]{0:T(128)S(1)}, s32[64]{0:T(128)}, u32[]{:S(2)}) copy-start(s32[64]{0:T(128)} %param.14) | copy-start | bytes 772
  10.5 22.4 %copy-start.5 = (f32[512]{0:T(512)S(1)}, f32[512]{0:T(512)}, u32[]{:S(2)}) copy-start(f32[512]{0:T(512)} %param.18) | copy-start | bytes 6148
  10.5 37.4 %copy-start.3 = (bf16[48,576]{1,0:T(8,128)(2,1)S(1)}, bf16[48,576]{1,0:T(8,128)(2,1)}, u32[]{:S(2)}) copy-start(bf16[48,576]{1,0:T(8,128)(2,1)} %param.12) | copy-start | bytes 165892
  10.5 51.2 %copy-start.4 = (f32[1536]{0:T(1024)S(1)}, f32[1536]{0:T(1024)}, u32[]{:S(2)}) copy-start(f32[1536]{0:T(1024)} %param.17) | copy-start | bytes 18436
  10.5 50.1 %reduce-scatter.5.cloned.1.call-start = ((), (), s32[]{:S(2)}) async-start(), calls=%async_computation.3 | async-start | bytes 491520 | tf_op jit(solution)/shard_map/reduce_scatter | solution.py:89
  33.7 2.2 %collective-permute-start = (bf16[16,576]{1,0:T(8,128)(2,1)S(1)}, bf16[16,576]{1,0:T(8,128)(2,1)S(1)}, u32[]{:S(2)}, u32[]{:S(2)}) collective-permute-start(bf16[16,576]{1,0:T(8,128)(2,1)S(1)} %pad_maximum_fusion.2), channel_id=1, source_target_pairs={{0,1},{1,2},{2,3},{3,0},{4,5},{5,6},{6,7},{7,4},{8,9},{9,10},{10,1... | collective-permute-start | bytes 55304 | tf_op jit(solution)/shard_map/ppermute | solution.py:19
  35.9 3.2 %collective-permute-start.1 = (bf16[16,576]{1,0:T(8,128)(2,1)S(1)}, bf16[16,576]{1,0:T(8,128)(2,1)S(1)}, u32[]{:S(2)}, u32[]{:S(2)}) collective-permute-start(bf16[16,576]{1,0:T(8,128)(2,1)S(1)} %collective-permute-done), channel_id=1, source_target_pairs={{0,1},{1,2},{2,3},{3,0},{4,5},{5,6},{6,7},{7,4},{8,9},{9,10},{10,1... | collective-permute-start | bytes 55304 | tf_op jit(solution)/shard_map/ppermute | solution.py:19
  38.4 3.2 %collective-permute-start.2 = (bf16[16,576]{1,0:T(8,128)(2,1)S(1)}, bf16[16,576]{1,0:T(8,128)(2,1)S(1)}, u32[]{:S(2)}, u32[]{:S(2)}) collective-permute-start(bf16[16,576]{1,0:T(8,128)(2,1)S(1)} %pad_maximum_fusion.2), channel_id=1, source_target_pairs={{0,3},{1,0},{2,1},{3,2},{4,7},{5,4},{6,5},{7,6},{8,11},{9,8},{10,9... | collective-permute-start | bytes 55304 | tf_op jit(solution)/shard_map/ppermute | solution.py:21
  41.8 6.0 %collective-permute-start.3 = (bf16[64,576]{1,0:T(8,128)(2,1)S(1)}, bf16[64,576]{1,0:T(8,128)(2,1)S(1)}, u32[]{:S(2)}, u32[]{:S(2)}) collective-permute-start(bf16[64,576]{1,0:T(8,128)(2,1)S(1)} %get-tuple-element.10), channel_id=1, source_target_pairs={{0,16},{1,17},{2,18},{3,19},{4,20},{5,21},{6,22},{7,23},{8,24},{9,... | collective-permute-start | bytes 221192 | tf_op jit(solution)/shard_map/ppermute | solution.py:29
  86.7 3.5 %copy-start.1 = (bf16[32,128,512]{2,1,0:T(8,128)(2,1)S(1)}, bf16[32,128,512]{2,1,0:T(8,128)(2,1)}, u32[]{:S(2)}) copy-start(bf16[32,128,512]{2,1,0:T(8,128)(2,1)} %param.20) | copy-start | bytes 12582916
  101.0 2.2 %copy-start.2 = (bf16[32,512,128]{2,1,0:T(8,128)(2,1)S(1)}, bf16[32,512,128]{2,1,0:T(8,128)(2,1)}, u32[]{:S(2)}) copy-start(bf16[32,512,128]{2,1,0:T(8,128)(2,1)} %param.21) | copy-start | bytes 12582916
Sparse Core Ops, SparseCore 0:
  10.6 20.3 reduce-scatter.2
  33.5 21.1 reduce-scatter.4
